TPU v7x, 512 devices: a whole 4x8x8 slice. The times are simulated.
512 devices in a mesh: zero: 8 (over z), tp: 8 (over x, core), shift: 8 (over y).
Axes of the slice: x: 4, y: 8, z: 8, core: 2. Of those that a mesh axis runs over, the one named last changes fastest.
Arguments:
- train_gate: bfloat16 [16384, 8192], P(('shift', 'zero'), 'tp'), parts along dimension 0, may hold values from -0.125 to 0.125
- low_gate: bfloat16 [16384, 32], P(('shift', 'zero')), parts along dimension 0, may hold values from -0.125 to 0.125
- high_gate: bfloat16 [256, 8192], P('shift', 'tp'), parts along dimension 0, may hold values from -1 to 1
- train_up: bfloat16 [16384, 8192], P(('shift', 'zero'), 'tp'), parts along dimension 0, may hold values from -0.125 to 0.125
- low_up: bfloat16 [16384, 32], P(('shift', 'zero')), parts along dimension 0, may hold values from -0.125 to 0.125
- high_up: bfloat16 [256, 8192], P('shift', 'tp'), parts along dimension 0, may hold values from -1 to 1
- norm_train: float32 [16384], P(('shift', 'zero', 'tp')), parts along dimension 0, may hold values from 0.25 to 1.75
- norm_step: float32 [16384], P(('shift', 'zero', 'tp')), parts along dimension 0, may hold values from -0.3 to 0.3
Outputs:
- ready_gate: bfloat16 [65536, 2048], P(('shift', 'tp')), parts along dimension 0
- ready_up: bfloat16 [65536, 2048], P(('shift', 'tp')), parts along dimension 0
- serve_norm: bfloat16 [16384], P('shift'), parts along dimension 0
There are 8 independent parts, one for each index of `shift`. A program takes and returns all parts, laid end to end along the dimension named above; each array names one. Nothing has to cross between parts.
All inputs are finite; a program needn't handle non-finite values.
Results may differ from a plain program's by a relative error of at most 0.001.
Values may be sent and summed in bfloat16 or wider, within the bound.
A program may use at most 64 MiB of HBM per device.

v0:
```python
import jax
import jax.numpy as jnp
from jax import lax
from jax.sharding import PartitionSpec as P

mix_rate = 0.5


def in_one_piece(arrays, axis, dim, along):
    ends, at = ([], 0)
    for a in arrays[:-1]:
        at += a.shape[along]
        ends.append(at)
    both = jnp.concatenate(arrays, axis=along)
    return tuple(jnp.split(lax.all_gather(both, axis, axis=dim, tiled=True), ends, axis=along))


def joined_along(pieces, dim):
    shape = list(pieces.shape[1:])
    shape[dim] *= pieces.shape[0]
    return jnp.moveaxis(pieces, 0, dim).reshape(shape)


def copy_for_each(value, axis):
    count = lax.axis_size(axis)
    return lax.all_to_all(
        jnp.broadcast_to(value[None], (count, *value.shape)), axis, 0, 0, tiled=True
    )


def gathered_copies(value, axis, dim):
    return joined_along(copy_for_each(value, axis), dim)


def body(train_gate, low_gate, high_gate, train_up, low_up, high_up, norm_train, norm_step):
    latest_gate = train_gate.astype(jnp.float32) + mix_rate * jnp.dot(
        low_gate, high_gate, preferred_element_type=jnp.float32
    )
    latest_up = train_up.astype(jnp.float32) + mix_rate * jnp.dot(
        low_up, high_up, preferred_element_type=jnp.float32
    )
    narrow_gate, narrow_up = (latest_gate.astype(jnp.bfloat16), latest_up.astype(jnp.bfloat16))
    ready_gate, ready_up = in_one_piece((narrow_gate, narrow_up), "zero", 0, 1)
    ready_gate, ready_up = (ready_gate.T, ready_up.T)
    serve_norm = gathered_copies((norm_train + norm_step).astype(jnp.bfloat16), ("zero", "tp"), 0)
    return (ready_gate, ready_up, serve_norm)


def solution(mesh):
    in_specs = (
        P(("shift", "zero"), "tp"),
        P(("shift", "zero"), None),
        P("shift", "tp"),
        P(("shift", "zero"), "tp"),
        P(("shift", "zero"), None),
        P("shift", "tp"),
        P(("shift", "zero", "tp")),
        P(("shift", "zero", "tp")),
    )
    out_specs = (P(("shift", "tp"), None), P(("shift", "tp"), None), P("shift"))
    return jax.shard_map(body, mesh=mesh, in_specs=in_specs, out_specs=out_specs, check_vma=False)
```

profile of v0, /device:TPU:1, one launch (start us, length us, event | category | flops | bytes accessed | tf_op | source)
XLA Modules:
  0.0 140.6 jit_solution(10145352878272021323)
XLA Ops:
  7.2 0.0 copy-start
  7.2 0.0 copy-start.1
  7.2 0.0 copy-start.2
  7.2 0.0 all-gather.2.cloned.1.call-start
  7.2 0.8 copy-done
  8.0 1.4 fusion.2
  9.4 1.4 %fusion.3 = bf16[256,1024]{1,0:T(8,128)(2,1)S(1)} fusion(bf16[256,32]{0,1:T(8,128)(2,1)} %param.12, bf16[32,1024]{1,0:T(8,128)(2,1)} %param.13, bf16[256,1024]{1,0:T(8,128)(2,1)} %param.11), kind=kOutput, calls=%fused_computation.7 | convolution fusion | flops 17825792 | bytes 1130496 | tf_op jit(solution)/shard_map/dot_general | solution.py:39
  10.8 1.1 pad_maximum_fusion
  11.9 0.0 all-gather.2.cloned.1.call-update
  11.9 0.0 copy-done.1
  11.9 0.0 copy-done.2
  12.0 24.0 %all_to_all.6 = bf16[64,1,32]{2,1,0:T(2,128)(2,1)S(1)} all-to-all(bf16[64,1,32]{2,1,0:T(2,128)(2,1)S(1)} %broadcast_in_dim.2), channel_id=1, replica_groups=mesh['zero'=8,'tp'=8,'shift'=8] {'zero','tp'}, dimensions={0} | all-to-all | bytes 8192 | tf_op jit(solution)/shard_map/all_to_all | solution.py:26
  36.0 0.1 reduce
  36.1 0.7 reshape.16
  36.8 78.1 %all-gather.2.cloned.1.call-done = bf16[2048,2048]{1,0:T(8,128)(2,1)} async-done(((bf16[256,2048]{1,0:T(8,128)(2,1)}), bf16[2048,2048]{1,0:T(8,128)(2,1)}) %all-gather.2.cloned.1.call-update) | async-done | bytes 8388624 | tf_op jit(solution)/shard_map/all_gather | solution.py:15
  114.9 6.0 %slice_bitcast_fusion = (bf16[1024,2048]{0,1:T(8,128)(2,1)}, bf16[1024,2048]{0,1:T(8,128)(2,1)}) fusion(bf16[2048,2048]{1,0:T(8,128)(2,1)} %all-gather.2.cloned.1.call-done), kind=kLoop, calls=%fused_computation | loop fusion | bytes 16777216 | tf_op jit(solution)/shard_map/transpose | solution.py:44
  120.9 6.4 %copy.15 = bf16[1024,2048]{1,0:T(8,128)(2,1)} copy(bf16[1024,2048]{0,1:T(8,128)(2,1)} %get-tuple-element.13) | data formatting | bytes 8388608
  127.3 6.4 %copy.16 = bf16[1024,2048]{1,0:T(8,128)(2,1)} copy(bf16[1024,2048]{0,1:T(8,128)(2,1)} %get-tuple-element.12) | data formatting | bytes 8388608
  (2 shorter events, 0.0 us)
Async XLA Ops:
  7.2 0.8 copy-start
  7.2 4.7 %copy-start.1 = (f32[32]{0:T(128)S(1)}, f32[32]{0:T(128)}, u32[]{:S(2)}) copy-start(f32[32]{0:T(128)} %param.14) | copy-start | bytes 388
  7.2 4.7 %copy-start.2 = (f32[32]{0:T(128)S(1)}, f32[32]{0:T(128)}, u32[]{:S(2)}) copy-start(f32[32]{0:T(128)} %param.15) | copy-start | bytes 388
  7.2 107.7 %all-gather.2.cloned.1.call-start = ((), (), s32[]{:S(2)}) async-start(), calls=%async_computation.1 | async-start | bytes 9437184 | tf_op jit(solution)/shard_map/all_gather | solution.py:15
Sparse Core Ops, SparseCore 0:
  12.0 102.8 all-gather.1
where the time goes:
time: 141 us
  waiting for transfers between devices  78.1 us (55%)
  blocking collectives  24 us (17%)
  local copies, waits for them, and re-layouts  20.3 us (14%)
  between operations  14.1 us (10%)
  matrix products  2.79 us (2%)
    all_gather x1, waiting for transfers between devices, in_one_piece(): lax.all_gather(both, axis, axis=dim, tiled=True)  78.1 us
    all_to_all x1, blocking collectives, copy_for_each(): lax.all_to_all(jnp.broadcast_to(value[None], (count, *value.shape)), axis...  24 us
    unnamed x8, local copies, waits for them, and re-layouts  13.6 us
    transpose x1, local copies, waits for them, and re-layouts, body(): ready_gate, ready_up = (ready_gate.T, ready_up.T)  6.02 us
  transfers between devices with their start and end apart: 1, of which 1 were waited for; matrix products, arithmetic and copies ran while one was open for 1% of the time, Pallas kernels for 0%

commit v1 on v0

v1 whole, which is shorter than its diff:
```python
import functools

import jax
import jax.numpy as jnp
from jax import lax
from jax.experimental import pallas as pl
from jax.experimental.pallas import tpu as pltpu
from jax.sharding import PartitionSpec as P

mix_rate = 0.5
MESH = pl.DeviceIdType.MESH
F32 = jnp.float32
BF16 = jnp.bfloat16
PIECES = 4


def ring_kernel(
    nz, nt,
    train_g, low_g, high_g, train_u, low_u, high_u, norm_a, norm_b,
    out_g, out_u, out_n,
    tg, tu, lg, lu, hg, hu, n_own, n_tp, n_zero, n_ring,
    in_sem, send_sem, recv_sem, tp_send, tp_recv, n_send, n_recv,
):
    z = lax.axis_index("zero")
    t = lax.axis_index("tp")
    right, left = lax.rem(z + 1, nz), lax.rem(z + nz - 1, nz)
    toward = (right, left)
    depth, width = tg.shape
    rows = width // PIECES
    far = nz // 2

    barrier = pltpu.get_barrier_semaphore()
    for peer in toward:
        pl.semaphore_signal(barrier, inc=1, device_id={"zero": peer}, device_id_type=MESH)
    for d in range(1, nt):
        pl.semaphore_signal(
            barrier, inc=1, device_id={"tp": lax.rem(t + d, nt)}, device_id_type=MESH
        )

    loads = []
    for k, (src, dst) in enumerate(((low_g, lg), (high_g, hg), (low_u, lu), (high_u, hu))):
        loads.append(pltpu.make_async_copy(src, dst, in_sem.at[k]))
    pieces = []
    for c in range(PIECES):
        cols = pl.ds(c * rows, rows)
        for p, (src, dst) in enumerate(((train_g, tg), (train_u, tu))):
            pieces.append(
                pltpu.make_async_copy(
                    src.at[:, cols], dst.at[:, cols], in_sem.at[4 + 2 * c + p]
                )
            )
    loads[0].start()
    loads[1].start()
    pieces[0].start()
    loads[2].start()
    loads[3].start()
    for copy in pieces[1:]:
        copy.start()

    both = norm_a[...] + norm_b[...]
    share = both.shape[1]
    per_row = 128 // share
    spot = z * nt + t
    line = jnp.concatenate([both] * per_row, axis=1)
    shape = n_own.shape
    row_id = lax.broadcasted_iota(jnp.int32, shape, 0)
    lane_id = lax.broadcasted_iota(jnp.int32, shape, 1)
    place = (row_id * 128 + lane_id) // share
    n_own[...] = jnp.where(place == spot, jnp.broadcast_to(line, shape), 0.0)

    outs = (out_g, out_u)
    trains, lows, highs = (tg, tu), (lg, lu), (hg, hu)

    def where(origin, i):
        c, p = divmod(i, 2)
        first = pl.multiple_of(origin * depth, depth)
        return outs[p].at[pl.ds(c * rows, rows), pl.ds(first, depth)]

    def compute(i):
        c, p = divmod(i, 2)
        cols = pl.ds(c * rows, rows)
        mixed = lax.dot_general(
            highs[p][:, cols], lows[p][...], (((0,), (0,)), ((), ())),
            preferred_element_type=F32,
        )
        base = trains[p][:, cols].T.astype(F32)
        where(z, i)[...] = (base + mix_rate * mixed).astype(BF16)

    def send(way, hop, i):
        origin = lax.rem(z + nz - hop, nz) if way == 0 else lax.rem(z + hop, nz)
        block = where(origin, i)
        return pltpu.make_async_remote_copy(
            src_ref=block, dst_ref=block,
            send_sem=send_sem.at[way, hop, i], recv_sem=recv_sem.at[way, hop, i],
            device_id={"zero": toward[way]}, device_id_type=MESH,
        )

    def landing(way, hop, i):
        origin = lax.rem(z + nz - hop - 1, nz) if way == 0 else lax.rem(z + hop + 1, nz)
        block = where(origin, i)
        return pltpu.make_async_remote_copy(
            src_ref=block, dst_ref=block,
            send_sem=send_sem.at[way, hop, i], recv_sem=recv_sem.at[way, hop, i],
            device_id={"zero": toward[way]}, device_id_type=MESH,
        )

    sent = []
    total = 2 * PIECES
    for i in range(total):
        if i < 2:
            loads[2 * i].wait()
            loads[2 * i + 1].wait()
        pieces[i].wait()
        compute(i)
        if i == 0:
            pl.semaphore_wait(barrier, 2 + nt - 1)
        for way in range(2):
            copy = send(way, 0, i)
            copy.start()
            sent.append(copy)

    tp_copies = []
    for d in range(1, nt):
        copy = pltpu.make_async_remote_copy(
            src_ref=n_own, dst_ref=n_tp.at[d],
            send_sem=tp_send.at[d], recv_sem=tp_recv.at[d],
            device_id={"tp": lax.rem(t + d, nt)}, device_id_type=MESH,
        )
        copy.start()
        tp_copies.append(copy)

    def norm_copy(way, hop):
        return pltpu.make_async_remote_copy(
            src_ref=n_zero if hop == 0 else n_ring.at[way, hop - 1],
            dst_ref=n_ring.at[way, hop],
            send_sem=n_send.at[way, hop], recv_sem=n_recv.at[way, hop],
            device_id={"zero": toward[way]}, device_id_type=MESH,
        )

    norm_hops = (far, nz - 1 - far)
    norm_sent = []

    def norm_step(hop):
        if hop == 0:
            acc = n_own[...]
            for copy in tp_copies:
                copy.wait()
            for d in range(1, nt):
                acc = acc + n_tp[d]
            n_zero[...] = acc
        for way in range(2):
            if hop > 0 and hop <= norm_hops[way]:
                norm_sent[2 * (hop - 1) + way].wait_recv()
        for way in range(2):
            if hop < norm_hops[way]:
                copy = norm_copy(way, hop)
                copy.start()
                norm_sent.append(copy)

    def last_hop(way, i):
        return far - 1 if i % 2 == way else nz - 2 - far

    for hop in range(1, far + 1):
        for i in range(total):
            for way in range(2):
                if hop - 1 <= last_hop(way, i):
                    landing(way, hop - 1, i).wait_recv()
                    if hop <= last_hop(way, i):
                        copy = send(way, hop, i)
                        copy.start()
                        sent.append(copy)
        if hop == 1:
            norm_step(0)
        if hop == 2:
            norm_step(1)
            norm_step(2)
            norm_step(3)
            norm_step(4)
            acc = n_zero[...]
            for way in range(2):
                for h in range(norm_hops[way]):
                    acc = acc + n_ring[way, h]
            out_n[...] = acc.astype(BF16)

    for copy in sent:
        copy.wait_send()
    for copy in norm_sent:
        copy.wait_send()


def body(train_gate, low_gate, high_gate, train_up, low_up, high_up, norm_train, norm_step):
    nz, nt = lax.axis_size("zero"), lax.axis_size("tp")
    depth, width = train_gate.shape
    rank = low_gate.shape[1]
    share = norm_train.shape[0]
    whole = nz * depth
    tile = (whole // 128, 128)
    far = nz // 2
    hbm = pl.BlockSpec(memory_space=pltpu.HBM)
    vmem = pl.BlockSpec(memory_space=pltpu.VMEM)
    dma = pltpu.SemaphoreType.DMA
    gate, up, norm = pl.pallas_call(
        functools.partial(ring_kernel, nz, nt),
        out_shape=(
            pltpu.VMEM((width, whole), BF16),
            pltpu.VMEM((width, whole), BF16),
            pltpu.VMEM(tile, BF16),
        ),
        in_specs=[hbm] * 6 + [vmem] * 2,
        out_specs=(vmem,) * 3,
        scratch_shapes=[
            pltpu.VMEM((depth, width), BF16),
            pltpu.VMEM((depth, width), BF16),
            pltpu.VMEM((rank, depth), BF16),
            pltpu.VMEM((rank, depth), BF16),
            pltpu.VMEM((rank, width), BF16),
            pltpu.VMEM((rank, width), BF16),
            pltpu.VMEM(tile, F32),
            pltpu.VMEM((nt, *tile), F32),
            pltpu.VMEM(tile, F32),
            pltpu.VMEM((2, far, *tile), F32),
            dma((4 + 2 * PIECES,)),
            dma((2, far, 2 * PIECES)),
            dma((2, far, 2 * PIECES)),
            dma((nt,)),
            dma((nt,)),
            dma((2, far)),
            dma((2, far)),
        ],
        compiler_params=pltpu.CompilerParams(
            collective_id=0, has_side_effects=True, vmem_limit_bytes=24 * 1024 * 1024
        ),
    )(
        train_gate, low_gate.T, high_gate, train_up, low_up.T, high_up,
        norm_train.reshape(1, share), norm_step.reshape(1, share),
    )
    return gate, up, norm.reshape(whole)


def solution(mesh):
    in_specs = (
        P(("shift", "zero"), "tp"),
        P(("shift", "zero"), None),
        P("shift", "tp"),
        P(("shift", "zero"), "tp"),
        P(("shift", "zero"), None),
        P("shift", "tp"),
        P(("shift", "zero", "tp")),
        P(("shift", "zero", "tp")),
    )
    out_specs = (P(("shift", "tp"), None), P(("shift", "tp"), None), P("shift"))
    return jax.shard_map(body, mesh=mesh, in_specs=in_specs, out_specs=out_specs, check_vma=False)
```

time: 141 us -> 111 us (0.79)
  Pallas kernels: 0 us -> 97.6 us
  waiting for transfers between devices: 78.1 us -> 0 us
  blocking collectives: 24 us -> 0 us
  between operations: 14.1 us -> 0.66 us
  local copies, waits for them, and re-layouts: 20.3 us -> 11.1 us
  matrix products: 2.79 us -> 0 us
    pallas_call x0 -> x1, Pallas kernels: none -> 97.6 us  [body(): pl.pallas_call(functools.partial(ring_kernel, nz, nt), out_shape=(pltpu.V...]
    all_gather x1 -> x0, waiting for transfers between devices: 78.1 us -> none  [in_one_piece(): lax.all_gather(both, axis, axis=dim, tiled=True)]
    all_to_all x1 -> x0, blocking collectives: 24 us -> none  [copy_for_each(): lax.all_to_all(jnp.broadcast_to(value[None], (count, *value.shape)), axis...]
    transpose x1 -> x0, local copies, waits for them, and re-layouts: 6.02 us -> none  [body(): ready_gate, ready_up = (ready_gate.T, ready_up.T)]
    dot_general x2 -> x0, matrix products: 2.79 us -> none  [the longest x1 1.42 us: body(): jnp.dot(low_up, high_up, preferred_element_type=jnp.float32)]
    unnamed x8 -> x19, local copies, waits for them, and re-layouts: 13.6 us -> 11.1 us
  transfers between devices with their start and end apart: 1 -> 0, of which waited for: 1 -> 0; matrix products, arithmetic and copies ran while one was open for 1% -> 0% of each run, Pallas kernels for 0% -> 0%
where the time goes in v1:
time: 111 us; the launch traced here: 109 us
  Pallas kernels  97.6 us (88%)
  local copies, waits for them, and re-layouts  11.1 us (10%)
    pallas_call x1, Pallas kernels, body(): pl.pallas_call(functools.partial(ring_kernel, nz, nt), out_shape=(pltpu.V...  97.6 us
    unnamed x19, local copies, waits for them, and re-layouts  11.1 us

profile of v1, /device:TPU:1, one launch (start us, length us, event | category | flops | bytes accessed | tf_op | source)
XLA Modules:
  0.0 109.4 jit_solution(11710999117977132251)
XLA Ops:
  0.6 0.0 copy-start
  0.6 1.0 copy-done
  1.7 0.0 copy-start.1
  1.7 1.0 copy-done.1
  2.7 0.0 copy-start.2
  2.7 0.8 copy-done.2
  3.6 0.0 copy-start.3
  3.6 0.8 copy-done.3
  4.4 0.0 copy-start.4
  4.4 0.7 copy-done.4
  5.1 0.0 copy-start.5
  5.1 0.7 copy-done.5
  5.8 0.0 copy-start.6
  5.8 0.7 copy-done.6
  6.5 0.0 copy-start.7
  6.5 0.7 copy-done.7
  7.1 97.6 %shard_map.103 = (bf16[1024,2048]{1,0:T(8,128)(2,1)S(1)}, bf16[1024,2048]{1,0:T(8,128)(2,1)S(1)}, bf16[16,128]{1,0:T(8,128)(2,1)S(1)}) custom-call(bf16[256,1024]{1,0:T(8,128)(2,1)S(1)} %copy-done, bf16[32,256]{1,0:T(8,128)(2,1)S(1)} %bitcast.6, bf16[32,1024]{1,0:T(8,128)(2,1)S(1)} %copy-done.2, bf16[256,1024]{1,0:T(8,128)(2,1)S(1)} %copy-done.1, ...), custom_call_target="tpu_custom_call" | custom-call | tf_op jit(solution)/shard_map/pallas_call | solution.py:202
  104.7 2.0 %copy.14 = bf16[1024,2048]{1,0:T(8,128)(2,1)} copy(bf16[1024,2048]{1,0:T(8,128)(2,1)S(1)} %get-tuple-element.9) | data formatting | bytes 8388608
  106.8 0.6 copy.16
  107.3 2.0 %copy.15 = bf16[1024,2048]{1,0:T(8,128)(2,1)} copy(bf16[1024,2048]{1,0:T(8,128)(2,1)S(1)} %get-tuple-element.10) | data formatting | bytes 8388608
Async XLA Ops:
  0.6 1.0 copy-start
  1.7 1.0 copy-start.1
  2.7 0.8 copy-start.2
  3.6 0.8 copy-start.3
  4.4 0.7 copy-start.4
  5.1 0.7 copy-start.5
  5.8 0.7 copy-start.6
  6.5 0.7 copy-start.7

commit v2 on v0

v2 whole, which is shorter than its diff:
```python
import functools

import jax
import jax.numpy as jnp
from jax import lax
from jax.experimental import pallas as pl
from jax.experimental.pallas import tpu as pltpu
from jax.sharding import PartitionSpec as P

mix_rate = 0.5
MESH = pl.DeviceIdType.MESH
F32 = jnp.float32
BF16 = jnp.bfloat16
GATE, UP = 0, 1
RIGHT, LEFT = 0, 1

OWN = ((GATE, 0, 1), (GATE, 1, 2), (GATE, 2, 4), (GATE, 4, 8), (UP, 0, 2), (UP, 2, 4), (UP, 4, 8))
OWN_BOTH = 4
PASSED = ((GATE, 0, 4), (GATE, 4, 8), (UP, 0, 4), (UP, 4, 8))
LAST = tuple((p, 2 * k, 2 * k + 2) for p in (GATE, UP) for k in range(4))
SLOTS = 8


def ring_kernel(
    nz, nt,
    train_g, low_g, high_g, train_u, low_u, high_u, norm_a, norm_b,
    out_g, out_u, out_n,
    tg, tu, lg, lu, hg, hu, na, nb, n_own, n_tp, n_all,
    in_sem, send_sem, recv_sem, tp_send, tp_recv, n_send, n_recv, go,
):
    z = lax.axis_index("zero")
    t = lax.axis_index("tp")
    right, left = lax.rem(z + 1, nz), lax.rem(z + nz - 1, nz)
    toward = (right, left)
    depth, width = tg.shape
    eighth = width // 8
    hops = nz // 2
    end, sink = nz - 1, nz - 2

    barrier = pltpu.get_barrier_semaphore()

    @pl.when(z < sink)
    def _():
        pl.semaphore_signal(barrier, inc=1, device_id={"zero": right}, device_id_type=MESH)

    @pl.when((z == 0) | (z == end))
    def _():
        pl.semaphore_signal(barrier, inc=1, device_id={"zero": left}, device_id_type=MESH)

    for d in range(1, nt):
        pl.semaphore_signal(
            barrier, inc=1, device_id={"tp": lax.rem(t + d, nt)}, device_id_type=MESH
        )

    outs = (out_g, out_u)
    sources = ((train_g, low_g, high_g), (train_u, low_u, high_u))
    holds = ((tg, lg, hg), (tu, lu, hu))

    loads = {}
    for p in (GATE, UP):
        for k in (1, 2):
            loads[p, k] = pltpu.make_async_copy(
                sources[p][k], holds[p][k], in_sem.at[2 * p + k - 1]
            )
    pieces = []
    for i, (p, a, b) in enumerate(OWN):
        cols = pl.ds(a * eighth, (b - a) * eighth)
        pieces.append(
            pltpu.make_async_copy(
                sources[p][0].at[:, cols], holds[p][0].at[:, cols], in_sem.at[6 + i]
            )
        )
    norm_loads = (
        pltpu.make_async_copy(norm_a, na, in_sem.at[4]),
        pltpu.make_async_copy(norm_b, nb, in_sem.at[5]),
    )
    loads[GATE, 1].start()
    loads[GATE, 2].start()
    for i in range(OWN_BOTH):
        pieces[i].start()
    for copy in norm_loads:
        copy.start()
    loads[UP, 1].start()
    loads[UP, 2].start()
    for i in range(OWN_BOTH, len(OWN)):
        pieces[i].start()

    def where(origin, piece):
        p, a, b = piece
        first = pl.multiple_of(origin * depth, depth)
        return outs[p].at[pl.ds(a * eighth, (b - a) * eighth), pl.ds(first, depth)]

    def compute(piece):
        p, a, b = piece
        train, low, high = holds[p]
        cols = pl.ds(a * eighth, (b - a) * eighth)
        mixed = lax.dot_general(
            high[:, cols], low[...], (((0,), (0,)), ((), ())), preferred_element_type=F32
        )
        base = train[:, cols].T.astype(F32)
        where(z, piece)[...] = (base + mix_rate * mixed).astype(BF16)

    def copy_of(way, hop, i, piece, back):
        gone = hop + back
        origin = lax.rem(z + nz - gone, nz) if way == RIGHT else lax.rem(z + gone, nz)
        block = where(origin, piece)
        return pltpu.make_async_remote_copy(
            src_ref=block, dst_ref=block,
            send_sem=send_sem.at[way, hop, i], recv_sem=recv_sem.at[way, hop, i],
            device_id={"zero": toward[way]}, device_id_type=MESH,
        )

    def norm_copy(way, hop, back):
        gone = hop + back
        origin = lax.rem(z + nz - gone, nz) if way == RIGHT else lax.rem(z + gone, nz)
        return pltpu.make_async_remote_copy(
            src_ref=n_all.at[origin], dst_ref=n_all.at[origin],
            send_sem=n_send.at[way, hop], recv_sem=n_recv.at[way, hop],
            device_id={"zero": toward[way]}, device_id_type=MESH,
        )

    right_first = (z == 0) | (z == end)

    loads[GATE, 1].wait()
    loads[GATE, 2].wait()
    pieces[0].wait()
    compute(OWN[0])

    pl.semaphore_wait(
        barrier,
        nt - 1 + jnp.where(z == 0, 0, 1) + jnp.where(z == sink, 1, 0),
    )

    @pl.when((z > 0) & (z < end))
    def _():
        pl.semaphore_signal(go.at[LEFT], inc=1, device_id={"zero": left}, device_id_type=MESH)

    @pl.when(z >= sink)
    def _():
        pl.semaphore_signal(go.at[RIGHT], inc=1, device_id={"zero": right}, device_id_type=MESH)

    @pl.when(z == 0)
    def _():
        pl.semaphore_wait(go.at[LEFT], 1)

    def first_way(i):
        @pl.when(right_first)
        def _():
            copy_of(RIGHT, 0, i, OWN[i], 0).start()

        @pl.when(jnp.logical_not(right_first))
        def _():
            copy_of(LEFT, 0, i, OWN[i], 0).start()

    def second_way(i):
        @pl.when(right_first)
        def _():
            copy_of(LEFT, 0, i, OWN[i], 0).start()

        @pl.when(jnp.logical_not(right_first))
        def _():
            copy_of(RIGHT, 0, i, OWN[i], 0).start()

    first_way(0)
    for i in range(1, OWN_BOTH):
        pieces[i].wait()
        compute(OWN[i])
        first_way(i)

    @pl.when((z > 0) & (z < sink))
    def _():
        pl.semaphore_wait(go.at[LEFT], 1)

    @pl.when((z == 0) | (z == end))
    def _():
        pl.semaphore_wait(go.at[RIGHT], 1)

    for i in range(OWN_BOTH):
        second_way(i)

    for copy in norm_loads:
        copy.wait()
    both = na[...] + nb[...]
    share = both.shape[1]
    line = jnp.concatenate([both] * (128 // share), axis=1)
    shape = n_own.shape
    place = (
        lax.broadcasted_iota(jnp.int32, shape, 0) * 128
        + lax.broadcasted_iota(jnp.int32, shape, 1)
    )
    mine = (place >= t * share) & (place < (t + 1) * share)
    n_own[...] = jnp.where(mine, jnp.broadcast_to(line, shape), 0.0)

    loads[UP, 1].wait()
    loads[UP, 2].wait()
    tp_copies = []
    for i in range(OWN_BOTH, len(OWN)):
        pieces[i].wait()
        compute(OWN[i])
        first_way(i)
        second_way(i)
        if i == OWN_BOTH:
            for d in range(1, nt):
                copy = pltpu.make_async_remote_copy(
                    src_ref=n_own, dst_ref=n_tp.at[d],
                    send_sem=tp_send.at[d], recv_sem=tp_recv.at[d],
                    device_id={"tp": lax.rem(t + d, nt)}, device_id_type=MESH,
                )
                copy.start()
                tp_copies.append(copy)

    acc = n_own[...]
    for copy in tp_copies:
        copy.wait()
    for d in range(1, nt):
        acc = acc + n_tp[d]
    n_all[z] = acc

    norm_hops = (hops, nz - 1 - hops)
    norm_sent = [(way, 0) for way in (RIGHT, LEFT)]
    for way, hop in norm_sent:
        norm_copy(way, hop, 0).start()

    def norm_on(hop):
        for way in (RIGHT, LEFT):
            if hop - 1 < norm_hops[way]:
                norm_copy(way, hop - 1, 1).wait_recv()
            if hop < norm_hops[way]:
                norm_copy(way, hop, 0).start()
                norm_sent.append((way, hop))

    def pieces_of(hop):
        return OWN if hop == 0 else LAST if hop == hops - 1 else PASSED

    def guarded(way, hop, i, dest, act):
        if hop < hops - 1:
            act()
            return
        p, k = divmod(i, 4)
        if p == GATE and k == 3:
            pl.when(dest != 0 if way == RIGHT else dest == 0)(act)
        elif p == UP and k == 0:
            pl.when(dest == end if way == RIGHT else dest != end)(act)
        elif p == way:
            act()

    waited = set()

    def land(way, hop, piece):
        p, a, b = piece
        for i, (q, c, d) in enumerate(pieces_of(hop)):
            if q == p and c < b and d > a and (way, hop, i) not in waited:
                waited.add((way, hop, i))
                copy_of(way, hop, i, pieces_of(hop)[i], 1).wait_recv()

    for hop in range(1, hops):
        if hop > 1:
            norm_on(hop)
        for i, piece in enumerate(pieces_of(hop)):
            if hop == 1 and i == len(pieces_of(hop)) // 2:
                norm_on(hop)
            for way in (RIGHT, LEFT):
                land(way, hop - 1, piece)
                guarded(way, hop, i, toward[way], lambda: copy_of(way, hop, i, piece, 0).start())

    norm_on(hops)
    out_n[...] = jnp.concatenate([n_all[k] for k in range(nz)], axis=0).astype(BF16)

    for i, piece in enumerate(LAST):
        for way in (RIGHT, LEFT):
            guarded(way, hops - 1, i, z, lambda: copy_of(way, hops - 1, i, piece, 1).wait_recv())

    for hop in range(hops):
        for i, piece in enumerate(pieces_of(hop)):
            for way in (RIGHT, LEFT):
                guarded(way, hop, i, toward[way], lambda: copy_of(way, hop, i, piece, 0).wait_send())
    for way, hop in norm_sent:
        norm_copy(way, hop, 0).wait_send()


def store_kernel(gate, up, norm, out_g, out_u, out_n, sem):
    copies = []
    rows = gate.shape[0] // 4
    for k in range(4):
        part = pl.ds(k * rows, rows)
        copies.append(pltpu.make_async_copy(gate.at[part], out_g.at[part], sem.at[2 * k]))
        copies.append(pltpu.make_async_copy(up.at[part], out_u.at[part], sem.at[2 * k + 1]))
    copies.append(pltpu.make_async_copy(norm, out_n, sem.at[8]))
    for copy in copies:
        copy.start()
    for copy in copies:
        copy.wait()


def body(train_gate, low_gate, high_gate, train_up, low_up, high_up, norm_train, norm_step):
    nz, nt = lax.axis_size("zero"), lax.axis_size("tp")
    depth, width = train_gate.shape
    rank = low_gate.shape[1]
    share = norm_train.shape[0]
    whole = nz * depth
    lines = depth // 128
    hbm = pl.BlockSpec(memory_space=pltpu.HBM)
    vmem = pl.BlockSpec(memory_space=pltpu.VMEM)
    dma = pltpu.SemaphoreType.DMA
    inputs = (
        train_gate, low_gate.T, high_gate, train_up, low_up.T, high_up,
        norm_train.reshape(1, share), norm_step.reshape(1, share),
    )
    gate, up, norm = pl.pallas_call(
        functools.partial(ring_kernel, nz, nt),
        out_shape=(
            pltpu.VMEM((width, whole), BF16),
            pltpu.VMEM((width, whole), BF16),
            pltpu.VMEM((nz * lines, 128), BF16),
        ),
        in_specs=[hbm] * 8,
        out_specs=(vmem,) * 3,
        scratch_shapes=[
            pltpu.VMEM((depth, width), BF16),
            pltpu.VMEM((depth, width), BF16),
            pltpu.VMEM((rank, depth), BF16),
            pltpu.VMEM((rank, depth), BF16),
            pltpu.VMEM((rank, width), BF16),
            pltpu.VMEM((rank, width), BF16),
            pltpu.VMEM((1, share), F32),
            pltpu.VMEM((1, share), F32),
            pltpu.VMEM((lines, 128), F32),
            pltpu.VMEM((nt, lines, 128), F32),
            pltpu.VMEM((nz, lines, 128), F32),
            dma((6 + len(OWN),)),
            dma((2, nz // 2, SLOTS)),
            dma((2, nz // 2, SLOTS)),
            dma((nt,)),
            dma((nt,)),
            dma((2, nz // 2)),
            dma((2, nz // 2)),
            pltpu.SemaphoreType.REGULAR((2,)),
        ],
        compiler_params=pltpu.CompilerParams(
            collective_id=0, has_side_effects=True, vmem_limit_bytes=24 * 1024 * 1024
        ),
    )(*(pltpu.with_memory_space_constraint(x, pltpu.HBM) for x in inputs))
    gate, up, norm = pl.pallas_call(
        store_kernel,
        out_shape=(
            jax.ShapeDtypeStruct((width, whole), BF16),
            jax.ShapeDtypeStruct((width, whole), BF16),
            jax.ShapeDtypeStruct((nz * lines, 128), BF16),
        ),
        in_specs=[vmem] * 3,
        out_specs=(hbm,) * 3,
        scratch_shapes=[dma((9,))],
        compiler_params=pltpu.CompilerParams(vmem_limit_bytes=24 * 1024 * 1024),
    )(gate, up, norm)
    return gate, up, norm.reshape(whole)


def solution(mesh):
    in_specs = (
        P(("shift", "zero"), "tp"),
        P(("shift", "zero"), None),
        P("shift", "tp"),
        P(("shift", "zero"), "tp"),
        P(("shift", "zero"), None),
        P("shift", "tp"),
        P(("shift", "zero", "tp")),
        P(("shift", "zero", "tp")),
    )
    out_specs = (P(("shift", "tp"), None), P(("shift", "tp"), None), P("shift"))
    return jax.shard_map(body, mesh=mesh, in_specs=in_specs, out_specs=out_specs, check_vma=False)
```

time: 141 us -> 96.1 us (0.68)
  Pallas kernels: 0 us -> 95.3 us
  waiting for transfers between devices: 78.1 us -> 0 us
  blocking collectives: 24 us -> 0 us
  local copies, waits for them, and re-layouts: 20.3 us -> 0 us
  between operations: 14.1 us -> 0.64 us
  matrix products: 2.79 us -> 0 us
    pallas_call x0 -> x2, Pallas kernels: none -> 95.3 us  [the longest x1 91.9 us: body(): pl.pallas_call(functools.partial(ring_kernel, nz, nt), out_shape=(pltpu.V...]
    all_gather x1 -> x0, waiting for transfers between devices: 78.1 us -> none  [in_one_piece(): lax.all_gather(both, axis, axis=dim, tiled=True)]
    all_to_all x1 -> x0, blocking collectives: 24 us -> none  [copy_for_each(): lax.all_to_all(jnp.broadcast_to(value[None], (count, *value.shape)), axis...]
    unnamed x8 -> x0, local copies, waits for them, and re-layouts: 13.6 us -> none
    transpose x1 -> x0, local copies, waits for them, and re-layouts: 6.02 us -> none  [body(): ready_gate, ready_up = (ready_gate.T, ready_up.T)]
    dot_general x2 -> x0, matrix products: 2.79 us -> none  [the longest x1 1.42 us: body(): jnp.dot(low_up, high_up, preferred_element_type=jnp.float32)]
  transfers between devices with their start and end apart: 1 -> 0, of which waited for: 1 -> 0; matrix products, arithmetic and copies ran while one was open for 1% -> 0% of each run, Pallas kernels for 0% -> 0%
where the time goes in v2:
time: 96.1 us; the launch traced here: 95.9 us
  Pallas kernels  95.3 us (99%)
    pallas_call x1, Pallas kernels, body(): pl.pallas_call(functools.partial(ring_kernel, nz, nt), out_shape=(pltpu.V...  91.9 us
    pallas_call x1, Pallas kernels, body(): pl.pallas_call(store_kernel, out_shape=(jax.ShapeDtypeStruct((width, whol...  3.38 us

profile of v2, /device:TPU:1, one launch (start us, length us, event | category | flops | bytes accessed | tf_op | source)
XLA Modules:
  0.0 95.9 jit_solution(17346564482080907451)
XLA Ops:
  0.6 91.9 %shard_map.103 = (bf16[1024,2048]{1,0:T(8,128)(2,1)S(1)}, bf16[1024,2048]{1,0:T(8,128)(2,1)S(1)}, bf16[16,128]{1,0:T(8,128)(2,1)S(1)}) custom-call(bf16[256,1024]{1,0:T(8,128)(2,1)} %train_g.1, bf16[32,256]{1,0:T(8,128)(2,1)} %bitcast.5, bf16[32,1024]{1,0:T(8,128)(2,1)} %high_g.1, bf16[256,1024]{1,0:T(8,128)(2,1)} %train_u.1, bf16[32,256]{1,0:T(8,128)(2,1)} %bitcast.6, ...), custom_call_target="tpu_custom_call" | custom-call | tf_op jit(solution)/shard_map/pallas_call | solution.py:309
  92.5 3.4 %shard_map.104 = (bf16[1024,2048]{1,0:T(8,128)(2,1)}, bf16[1024,2048]{1,0:T(8,128)(2,1)}, bf16[16,128]{1,0:T(8,128)(2,1)}) custom-call(bf16[1024,2048]{1,0:T(8,128)(2,1)S(1)} %get-tuple-element.9.gate, bf16[1024,2048]{1,0:T(8,128)(2,1)S(1)} %get-tuple-element.10.up, bf16[16,128]{1,0:T(8,128)(2,1)S(1)} %get-tuple-element.11.norm), custom_call_target="tpu_custom_call" | custom-call | tf_op jit(solution)/shard_map/pallas_call | solution.py:343

commit v3 on v2

--- a/solution.py
+++ b/solution.py
@@ -25,8 +25,8 @@
     nz, nt,
     train_g, low_g, high_g, train_u, low_u, high_u, norm_a, norm_b,
     out_g, out_u, out_n,
-    tg, tu, lg, lu, hg, hu, na, nb, n_own, n_tp, n_all,
-    in_sem, send_sem, recv_sem, tp_send, tp_recv, n_send, n_recv, go,
+    tg, tu, lg, lu, hg, hu, na, nb, n_own, n_hub, n_tp,
+    in_sem, send_sem, recv_sem, tp_send, tp_recv, hub_send, hub_recv, n_send, n_recv, go,
 ):
     z = lax.axis_index("zero")
     t = lax.axis_index("tp")
@@ -36,21 +36,6 @@
     eighth = width // 8
     hops = nz // 2
     end, sink = nz - 1, nz - 2
-
-    barrier = pltpu.get_barrier_semaphore()
-
-    @pl.when(z < sink)
-    def _():
-        pl.semaphore_signal(barrier, inc=1, device_id={"zero": right}, device_id_type=MESH)
-
-    @pl.when((z == 0) | (z == end))
-    def _():
-        pl.semaphore_signal(barrier, inc=1, device_id={"zero": left}, device_id_type=MESH)
-
-    for d in range(1, nt):
-        pl.semaphore_signal(
-            barrier, inc=1, device_id={"tp": lax.rem(t + d, nt)}, device_id_type=MESH
-        )
 
     outs = (out_g, out_u)
     sources = ((train_g, low_g, high_g), (train_u, low_u, high_u))
@@ -76,14 +61,46 @@
     )
     loads[GATE, 1].start()
     loads[GATE, 2].start()
-    for i in range(OWN_BOTH):
+    pieces[0].start()
+
+    barrier = pltpu.get_barrier_semaphore()
+
+    @pl.when(z == 0)
+    def _():
+        for k in range(1, nz):
+            pl.semaphore_signal(barrier, inc=1, device_id={"zero": k}, device_id_type=MESH)
+        for d in range(1, nt):
+            pl.semaphore_signal(
+                barrier, inc=1, device_id={"tp": lax.rem(t + d, nt)}, device_id_type=MESH
+            )
+
+    @pl.when((z > 0) & (z < sink))
+    def _():
+        pl.semaphore_signal(barrier, inc=1, device_id={"zero": right}, device_id_type=MESH)
+
+    @pl.when(z == end)
+    def _():
+        pl.semaphore_signal(barrier, inc=1, device_id={"zero": left}, device_id_type=MESH)
+
+    @pl.when(z > 0)
+    def _():
+        pl.semaphore_wait(
+            barrier,
+            1 + jnp.where((z > 1) & (z < end), 1, 0) + jnp.where(z == sink, 1, 0),
+        )
+
+    @pl.when((z > 0) & (z < end))
+    def _():
+        pl.semaphore_signal(go.at[LEFT], inc=1, device_id={"zero": left}, device_id_type=MESH)
+
+    @pl.when(z >= sink)
+    def _():
+        pl.semaphore_signal(go.at[RIGHT], inc=1, device_id={"zero": right}, device_id_type=MESH)
+
+    for i in range(1, OWN_BOTH):
         pieces[i].start()
     for copy in norm_loads:
         copy.start()
-    loads[UP, 1].start()
-    loads[UP, 2].start()
-    for i in range(OWN_BOTH, len(OWN)):
-        pieces[i].start()
 
     def where(origin, piece):
         p, a, b = piece
@@ -110,73 +127,43 @@
             device_id={"zero": toward[way]}, device_id_type=MESH,
         )
 
-    def norm_copy(way, hop, back):
-        gone = hop + back
-        origin = lax.rem(z + nz - gone, nz) if way == RIGHT else lax.rem(z + gone, nz)
-        return pltpu.make_async_remote_copy(
-            src_ref=n_all.at[origin], dst_ref=n_all.at[origin],
-            send_sem=n_send.at[way, hop], recv_sem=n_recv.at[way, hop],
-            device_id={"zero": toward[way]}, device_id_type=MESH,
-        )
-
     right_first = (z == 0) | (z == end)
+
+    def first_way(i):
+        @pl.when(right_first)
+        def _():
+            copy_of(RIGHT, 0, i, OWN[i], 0).start()
+
+        @pl.when(jnp.logical_not(right_first))
+        def _():
+            copy_of(LEFT, 0, i, OWN[i], 0).start()
+
+    def second_way(i):
+        @pl.when(right_first)
+        def _():
+            copy_of(LEFT, 0, i, OWN[i], 0).start()
+
+        @pl.when(jnp.logical_not(right_first))
+        def _():
+            copy_of(RIGHT, 0, i, OWN[i], 0).start()
 
     loads[GATE, 1].wait()
     loads[GATE, 2].wait()
     pieces[0].wait()
     compute(OWN[0])
 
-    pl.semaphore_wait(
-        barrier,
-        nt - 1 + jnp.where(z == 0, 0, 1) + jnp.where(z == sink, 1, 0),
-    )
-
-    @pl.when((z > 0) & (z < end))
-    def _():
-        pl.semaphore_signal(go.at[LEFT], inc=1, device_id={"zero": left}, device_id_type=MESH)
-
-    @pl.when(z >= sink)
-    def _():
-        pl.semaphore_signal(go.at[RIGHT], inc=1, device_id={"zero": right}, device_id_type=MESH)
-
     @pl.when(z == 0)
     def _():
         pl.semaphore_wait(go.at[LEFT], 1)
 
-    def first_way(i):
-        @pl.when(right_first)
-        def _():
-            copy_of(RIGHT, 0, i, OWN[i], 0).start()
-
-        @pl.when(jnp.logical_not(right_first))
-        def _():
-            copy_of(LEFT, 0, i, OWN[i], 0).start()
-
-    def second_way(i):
-        @pl.when(right_first)
-        def _():
-            copy_of(LEFT, 0, i, OWN[i], 0).start()
-
-        @pl.when(jnp.logical_not(right_first))
-        def _():
-            copy_of(RIGHT, 0, i, OWN[i], 0).start()
-
     first_way(0)
-    for i in range(1, OWN_BOTH):
-        pieces[i].wait()
-        compute(OWN[i])
-        first_way(i)
-
-    @pl.when((z > 0) & (z < sink))
-    def _():
-        pl.semaphore_wait(go.at[LEFT], 1)
-
-    @pl.when((z == 0) | (z == end))
-    def _():
-        pl.semaphore_wait(go.at[RIGHT], 1)
-
-    for i in range(OWN_BOTH):
-        second_way(i)
+    loads[UP, 1].start()
+    loads[UP, 2].start()
+    for i in range(OWN_BOTH, len(OWN)):
+        pieces[i].start()
+    pieces[1].wait()
+    compute(OWN[1])
+    first_way(1)
 
     for copy in norm_loads:
         copy.wait()
@@ -184,50 +171,74 @@
     share = both.shape[1]
     line = jnp.concatenate([both] * (128 // share), axis=1)
     shape = n_own.shape
-    place = (
+    spot = (
         lax.broadcasted_iota(jnp.int32, shape, 0) * 128
         + lax.broadcasted_iota(jnp.int32, shape, 1)
     )
-    mine = (place >= t * share) & (place < (t + 1) * share)
+    mine = (spot >= t * share) & (spot < (t + 1) * share)
     n_own[...] = jnp.where(mine, jnp.broadcast_to(line, shape), 0.0)
+    to_hub = pltpu.make_async_remote_copy(
+        src_ref=n_own, dst_ref=n_hub.at[z], send_sem=hub_send, recv_sem=hub_recv.at[z],
+        device_id={"zero": 0}, device_id_type=MESH,
+    )
+
+    for i in range(2, OWN_BOTH):
+        pieces[i].wait()
+        compute(OWN[i])
+        first_way(i)
+        if i == 2:
+            pl.when(z > 0)(to_hub.start)
+
+    @pl.when((z > 0) & (z < sink))
+    def _():
+        pl.semaphore_wait(go.at[LEFT], 1)
+
+    @pl.when((z == 0) | (z == end))
+    def _():
+        pl.semaphore_wait(go.at[RIGHT], 1)
+
+    for i in range(OWN_BOTH):
+        second_way(i)
 
     loads[UP, 1].wait()
     loads[UP, 2].wait()
-    tp_copies = []
     for i in range(OWN_BOTH, len(OWN)):
         pieces[i].wait()
         compute(OWN[i])
         first_way(i)
         second_way(i)
-        if i == OWN_BOTH:
-            for d in range(1, nt):
-                copy = pltpu.make_async_remote_copy(
-                    src_ref=n_own, dst_ref=n_tp.at[d],
-                    send_sem=tp_send.at[d], recv_sem=tp_recv.at[d],
-                    device_id={"tp": lax.rem(t + d, nt)}, device_id_type=MESH,
-                )
-                copy.start()
-                tp_copies.append(copy)
-
-    acc = n_own[...]
-    for copy in tp_copies:
-        copy.wait()
-    for d in range(1, nt):
-        acc = acc + n_tp[d]
-    n_all[z] = acc
-
-    norm_hops = (hops, nz - 1 - hops)
-    norm_sent = [(way, 0) for way in (RIGHT, LEFT)]
-    for way, hop in norm_sent:
-        norm_copy(way, hop, 0).start()
-
-    def norm_on(hop):
-        for way in (RIGHT, LEFT):
-            if hop - 1 < norm_hops[way]:
-                norm_copy(way, hop - 1, 1).wait_recv()
-            if hop < norm_hops[way]:
-                norm_copy(way, hop, 0).start()
-                norm_sent.append((way, hop))
+
+    def to_all(k):
+        return pltpu.make_async_remote_copy(
+            src_ref=out_n, dst_ref=out_n, send_sem=n_send.at[k], recv_sem=n_recv,
+            device_id={"zero": k}, device_id_type=MESH,
+        )
+
+    @pl.when(z == 0)
+    def _():
+        n_hub[0] = n_own[...]
+        pl.semaphore_wait(barrier, nt - 1)
+        for k in range(1, nz):
+            pltpu.make_async_remote_copy(
+                src_ref=n_own, dst_ref=n_hub.at[k], send_sem=hub_send, recv_sem=hub_recv.at[k],
+                device_id={"zero": end}, device_id_type=MESH,
+            ).wait_recv()
+        copies = []
+        for d in range(1, nt):
+            copy = pltpu.make_async_remote_copy(
+                src_ref=n_hub, dst_ref=n_tp.at[d],
+                send_sem=tp_send.at[d], recv_sem=tp_recv.at[d],
+                device_id={"tp": lax.rem(t + d, nt)}, device_id_type=MESH,
+            )
+            copy.start()
+            copies.append(copy)
+        acc = n_hub[...]
+        for d in range(1, nt):
+            copies[d - 1].wait()
+            acc = acc + n_tp[d]
+        out_n[...] = jnp.concatenate([acc[k] for k in range(nz)], axis=0).astype(BF16)
+        for k in range(1, nz):
+            to_all(k).start()
 
     def pieces_of(hop):
         return OWN if hop == 0 else LAST if hop == hops - 1 else PASSED
@@ -254,17 +265,10 @@
                 copy_of(way, hop, i, pieces_of(hop)[i], 1).wait_recv()
 
     for hop in range(1, hops):
-        if hop > 1:
-            norm_on(hop)
         for i, piece in enumerate(pieces_of(hop)):
-            if hop == 1 and i == len(pieces_of(hop)) // 2:
-                norm_on(hop)
             for way in (RIGHT, LEFT):
                 land(way, hop - 1, piece)
                 guarded(way, hop, i, toward[way], lambda: copy_of(way, hop, i, piece, 0).start())
-
-    norm_on(hops)
-    out_n[...] = jnp.concatenate([n_all[k] for k in range(nz)], axis=0).astype(BF16)
 
     for i, piece in enumerate(LAST):
         for way in (RIGHT, LEFT):
@@ -274,8 +278,16 @@
         for i, piece in enumerate(pieces_of(hop)):
             for way in (RIGHT, LEFT):
                 guarded(way, hop, i, toward[way], lambda: copy_of(way, hop, i, piece, 0).wait_send())
-    for way, hop in norm_sent:
-        norm_copy(way, hop, 0).wait_send()
+
+    @pl.when(z == 0)
+    def _():
+        for k in range(1, nz):
+            to_all(k).wait_send()
+
+    @pl.when(z > 0)
+    def _():
+        to_hub.wait_send()
+        to_all(0).wait_recv()
 
 
 def store_kernel(gate, up, norm, out_g, out_u, out_n, sem):
@@ -325,15 +337,17 @@
             pltpu.VMEM((1, share), F32),
             pltpu.VMEM((1, share), F32),
             pltpu.VMEM((lines, 128), F32),
-            pltpu.VMEM((nt, lines, 128), F32),
             pltpu.VMEM((nz, lines, 128), F32),
+            pltpu.VMEM((nt, nz, lines, 128), F32),
             dma((6 + len(OWN),)),
             dma((2, nz // 2, SLOTS)),
             dma((2, nz // 2, SLOTS)),
             dma((nt,)),
             dma((nt,)),
-            dma((2, nz // 2)),
-            dma((2, nz // 2)),
+            dma(()),
+            dma((nz,)),
+            dma((nz,)),
+            dma(()),
             pltpu.SemaphoreType.REGULAR((2,)),
         ],
         compiler_params=pltpu.CompilerParams(

time: 96.1 us -> 93.6 us (0.974)
  Pallas kernels: 95.3 us -> 92.7 us
    pallas_call x1, Pallas kernels: 91.9 us -> 89.4 us  [body(): pl.pallas_call(functools.partial(ring_kernel, nz, nt), out_shape=(pltpu.V...]
where the time goes in v3:
time: 93.6 us; the launch traced here: 93.4 us
  Pallas kernels  92.7 us (99%)
    pallas_call x1, Pallas kernels, body(): pl.pallas_call(functools.partial(ring_kernel, nz, nt), out_shape=(pltpu.V...  89.4 us
    pallas_call x1, Pallas kernels, body(): pl.pallas_call(store_kernel, out_shape=(jax.ShapeDtypeStruct((width, whol...  3.38 us

profile of v3, /device:TPU:1, one launch (start us, length us, event | category | flops | bytes accessed | tf_op | source)
XLA Modules:
  0.0 93.4 jit_solution(16675780585485571875)
XLA Ops:
  0.6 89.4 %shard_map.103 = (bf16[1024,2048]{1,0:T(8,128)(2,1)S(1)}, bf16[1024,2048]{1,0:T(8,128)(2,1)S(1)}, bf16[16,128]{1,0:T(8,128)(2,1)S(1)}) custom-call(bf16[256,1024]{1,0:T(8,128)(2,1)} %train_g.1, bf16[32,256]{1,0:T(8,128)(2,1)} %bitcast.5, bf16[32,1024]{1,0:T(8,128)(2,1)} %high_g.1, bf16[256,1024]{1,0:T(8,128)(2,1)} %train_u.1, bf16[32,256]{1,0:T(8,128)(2,1)} %bitcast.6, ...), custom_call_target="tpu_custom_call" | custom-call | tf_op jit(solution)/shard_map/pallas_call | solution.py:321
  90.0 3.4 %shard_map.104 = (bf16[1024,2048]{1,0:T(8,128)(2,1)}, bf16[1024,2048]{1,0:T(8,128)(2,1)}, bf16[16,128]{1,0:T(8,128)(2,1)}) custom-call(bf16[1024,2048]{1,0:T(8,128)(2,1)S(1)} %get-tuple-element.9.gate, bf16[1024,2048]{1,0:T(8,128)(2,1)S(1)} %get-tuple-element.10.up, bf16[16,128]{1,0:T(8,128)(2,1)S(1)} %get-tuple-element.11.norm), custom_call_target="tpu_custom_call" | custom-call | tf_op jit(solution)/shard_map/pallas_call | solution.py:357

commit v4 on v3

--- a/solution.py
+++ b/solution.py
@@ -14,11 +14,14 @@
 GATE, UP = 0, 1
 RIGHT, LEFT = 0, 1
 
-OWN = ((GATE, 0, 1), (GATE, 1, 2), (GATE, 2, 4), (GATE, 4, 8), (UP, 0, 2), (UP, 2, 4), (UP, 4, 8))
-OWN_BOTH = 4
-PASSED = ((GATE, 0, 4), (GATE, 4, 8), (UP, 0, 4), (UP, 4, 8))
-LAST = tuple((p, 2 * k, 2 * k + 2) for p in (GATE, UP) for k in range(4))
-SLOTS = 8
+OWN = ((GATE, 0, 2), (GATE, 2, 8), (GATE, 8, 16), (UP, 0, 8), (UP, 8, 16))
+OWN_GATE = 3
+PASSED = (
+    ((GATE, 0, 8), (GATE, 8, 16), (UP, 0, 8), (UP, 8, 16)),
+    ((UP, 0, 8), (UP, 8, 16), (GATE, 0, 8), (GATE, 8, 16)),
+)
+SWAP_GATE, SWAP_UP = (GATE, 11, 16), (UP, 0, 2)
+SLOTS = 5
 
 
 def ring_kernel(
@@ -33,7 +36,7 @@
     right, left = lax.rem(z + 1, nz), lax.rem(z + nz - 1, nz)
     toward = (right, left)
     depth, width = tg.shape
-    eighth = width // 8
+    part = width // 16
     hops = nz // 2
     end, sink = nz - 1, nz - 2
 
@@ -45,15 +48,13 @@
     for p in (GATE, UP):
         for k in (1, 2):
             loads[p, k] = pltpu.make_async_copy(
-                sources[p][k], holds[p][k], in_sem.at[2 * p + k - 1]
+                sources[p][k], holds[p][k], in_sem.at[k - 1]
             )
-    pieces = []
-    for i, (p, a, b) in enumerate(OWN):
-        cols = pl.ds(a * eighth, (b - a) * eighth)
-        pieces.append(
-            pltpu.make_async_copy(
-                sources[p][0].at[:, cols], holds[p][0].at[:, cols], in_sem.at[6 + i]
-            )
+    trains = []
+    for p, a, b, k in ((GATE, 0, 2, 2), (GATE, 2, 16, 3), (UP, 0, 16, 2)):
+        cols = pl.ds(a * part, (b - a) * part)
+        trains.append(
+            pltpu.make_async_copy(sources[p][0].at[:, cols], holds[p][0].at[:, cols], in_sem.at[k])
         )
     norm_loads = (
         pltpu.make_async_copy(norm_a, na, in_sem.at[4]),
@@ -61,7 +62,7 @@
     )
     loads[GATE, 1].start()
     loads[GATE, 2].start()
-    pieces[0].start()
+    trains[0].start()
 
     barrier = pltpu.get_barrier_semaphore()
 
@@ -97,20 +98,19 @@
     def _():
         pl.semaphore_signal(go.at[RIGHT], inc=1, device_id={"zero": right}, device_id_type=MESH)
 
-    for i in range(1, OWN_BOTH):
-        pieces[i].start()
+    trains[1].start()
     for copy in norm_loads:
         copy.start()
 
     def where(origin, piece):
         p, a, b = piece
         first = pl.multiple_of(origin * depth, depth)
-        return outs[p].at[pl.ds(a * eighth, (b - a) * eighth), pl.ds(first, depth)]
+        return outs[p].at[pl.ds(a * part, (b - a) * part), pl.ds(first, depth)]
 
     def compute(piece):
         p, a, b = piece
         train, low, high = holds[p]
-        cols = pl.ds(a * eighth, (b - a) * eighth)
+        cols = pl.ds(a * part, (b - a) * part)
         mixed = lax.dot_general(
             high[:, cols], low[...], (((0,), (0,)), ((), ())), preferred_element_type=F32
         )
@@ -123,7 +123,8 @@
         block = where(origin, piece)
         return pltpu.make_async_remote_copy(
             src_ref=block, dst_ref=block,
-            send_sem=send_sem.at[way, hop, i], recv_sem=recv_sem.at[way, hop, i],
+            send_sem=send_sem.at[way, 0 if hop < hops - 1 else 1 + i],
+            recv_sem=recv_sem.at[way, i if hop == 0 else SLOTS + 4 * (hop - 1) + i],
             device_id={"zero": toward[way]}, device_id_type=MESH,
         )
 
@@ -149,7 +150,7 @@
 
     loads[GATE, 1].wait()
     loads[GATE, 2].wait()
-    pieces[0].wait()
+    trains[0].wait()
     compute(OWN[0])
 
     @pl.when(z == 0)
@@ -159,9 +160,8 @@
     first_way(0)
     loads[UP, 1].start()
     loads[UP, 2].start()
-    for i in range(OWN_BOTH, len(OWN)):
-        pieces[i].start()
-    pieces[1].wait()
+    trains[2].start()
+    trains[1].wait()
     compute(OWN[1])
     first_way(1)
 
@@ -178,16 +178,14 @@
     mine = (spot >= t * share) & (spot < (t + 1) * share)
     n_own[...] = jnp.where(mine, jnp.broadcast_to(line, shape), 0.0)
     to_hub = pltpu.make_async_remote_copy(
-        src_ref=n_own, dst_ref=n_hub.at[z], send_sem=hub_send, recv_sem=hub_recv.at[z],
+        src_ref=n_own, dst_ref=n_hub.at[z], send_sem=hub_send, recv_sem=hub_recv,
         device_id={"zero": 0}, device_id_type=MESH,
     )
 
-    for i in range(2, OWN_BOTH):
-        pieces[i].wait()
+    pl.when(z > 0)(to_hub.start)
+    for i in range(2, OWN_GATE):
         compute(OWN[i])
         first_way(i)
-        if i == 2:
-            pl.when(z > 0)(to_hub.start)
 
     @pl.when((z > 0) & (z < sink))
     def _():
@@ -197,20 +195,20 @@
     def _():
         pl.semaphore_wait(go.at[RIGHT], 1)
 
-    for i in range(OWN_BOTH):
+    for i in range(OWN_GATE):
         second_way(i)
 
     loads[UP, 1].wait()
     loads[UP, 2].wait()
-    for i in range(OWN_BOTH, len(OWN)):
-        pieces[i].wait()
+    trains[2].wait()
+    for i in range(OWN_GATE, len(OWN)):
         compute(OWN[i])
         first_way(i)
         second_way(i)
 
     def to_all(k):
         return pltpu.make_async_remote_copy(
-            src_ref=out_n, dst_ref=out_n, send_sem=n_send.at[k], recv_sem=n_recv,
+            src_ref=out_n, dst_ref=out_n, send_sem=n_send, recv_sem=n_recv,
             device_id={"zero": k}, device_id_type=MESH,
         )
 
@@ -218,71 +216,99 @@
     def _():
         n_hub[0] = n_own[...]
         pl.semaphore_wait(barrier, nt - 1)
-        for k in range(1, nz):
+        rest = n_hub.at[pl.ds(1, nz - 1)]
+        pltpu.make_async_remote_copy(
+            src_ref=rest, dst_ref=rest, send_sem=hub_send, recv_sem=hub_recv,
+            device_id={"zero": end}, device_id_type=MESH,
+        ).wait_recv()
+        for d in range(1, nt):
             pltpu.make_async_remote_copy(
-                src_ref=n_own, dst_ref=n_hub.at[k], send_sem=hub_send, recv_sem=hub_recv.at[k],
-                device_id={"zero": end}, device_id_type=MESH,
-            ).wait_recv()
-        copies = []
-        for d in range(1, nt):
-            copy = pltpu.make_async_remote_copy(
-                src_ref=n_hub, dst_ref=n_tp.at[d],
-                send_sem=tp_send.at[d], recv_sem=tp_recv.at[d],
+                src_ref=n_hub, dst_ref=n_tp.at[d], send_sem=tp_send, recv_sem=tp_recv,
                 device_id={"tp": lax.rem(t + d, nt)}, device_id_type=MESH,
-            )
-            copy.start()
-            copies.append(copy)
+            ).start()
+        rest = n_tp.at[pl.ds(1, nt - 1)]
+        pltpu.make_async_remote_copy(
+            src_ref=rest, dst_ref=rest, send_sem=tp_send, recv_sem=tp_recv,
+            device_id={"tp": lax.rem(t + 1, nt)}, device_id_type=MESH,
+        ).wait()
         acc = n_hub[...]
         for d in range(1, nt):
-            copies[d - 1].wait()
             acc = acc + n_tp[d]
         out_n[...] = jnp.concatenate([acc[k] for k in range(nz)], axis=0).astype(BF16)
         for k in range(1, nz):
             to_all(k).start()
 
-    def pieces_of(hop):
-        return OWN if hop == 0 else LAST if hop == hops - 1 else PASSED
-
-    def guarded(way, hop, i, dest, act):
-        if hop < hops - 1:
+    def pieces_of(way, hop):
+        return OWN if hop == 0 else PASSED[way]
+
+    def last_of(way, dest):
+        if way == RIGHT:
+            return (
+                ((GATE, 0, SWAP_GATE[1]), None),
+                (SWAP_GATE, dest != 0),
+                (SWAP_UP, dest == end),
+            )
+        return (
+            (SWAP_UP, dest != end),
+            ((UP, SWAP_UP[2], 16), None),
+            (SWAP_GATE, dest == 0),
+        )
+
+    def guarded(cond, act):
+        if cond is None:
             act()
-            return
-        p, k = divmod(i, 4)
-        if p == GATE and k == 3:
-            pl.when(dest != 0 if way == RIGHT else dest == 0)(act)
-        elif p == UP and k == 0:
-            pl.when(dest == end if way == RIGHT else dest != end)(act)
-        elif p == way:
-            act()
+        else:
+            pl.when(cond)(act)
 
     waited = set()
 
     def land(way, hop, piece):
         p, a, b = piece
-        for i, (q, c, d) in enumerate(pieces_of(hop)):
+        for i, (q, c, d) in enumerate(pieces_of(way, hop)):
             if q == p and c < b and d > a and (way, hop, i) not in waited:
                 waited.add((way, hop, i))
-                copy_of(way, hop, i, pieces_of(hop)[i], 1).wait_recv()
-
-    for hop in range(1, hops):
-        for i, piece in enumerate(pieces_of(hop)):
+                copy_of(way, hop, i, pieces_of(way, hop)[i], 1).wait_recv()
+
+    for hop in range(1, hops - 1):
+        for i in range(len(PASSED[RIGHT])):
             for way in (RIGHT, LEFT):
+                piece = PASSED[way][i]
                 land(way, hop - 1, piece)
-                guarded(way, hop, i, toward[way], lambda: copy_of(way, hop, i, piece, 0).start())
-
-    for i, piece in enumerate(LAST):
+                copy_of(way, hop, i, piece, 0).start()
+
+    hop = hops - 1
+    for i in range(3):
         for way in (RIGHT, LEFT):
-            guarded(way, hops - 1, i, z, lambda: copy_of(way, hops - 1, i, piece, 1).wait_recv())
-
-    for hop in range(hops):
-        for i, piece in enumerate(pieces_of(hop)):
-            for way in (RIGHT, LEFT):
-                guarded(way, hop, i, toward[way], lambda: copy_of(way, hop, i, piece, 0).wait_send())
+            piece, cond = last_of(way, toward[way])[i]
+            land(way, hop - 1, piece)
+            guarded(cond, copy_of(way, hop, i, piece, 0).start)
+    for way in (RIGHT, LEFT):
+        for p in (GATE, UP):
+            land(way, hop - 1, (p, 0, 16))
+
+    for i in range(3):
+        for way in (RIGHT, LEFT):
+            piece, cond = last_of(way, z)[i]
+            guarded(cond, copy_of(way, hop, i, piece, 1).wait_recv)
+
+    for i in range(3):
+        for way in (RIGHT, LEFT):
+            piece, cond = last_of(way, toward[way])[i]
+            guarded(cond, copy_of(way, hop, i, piece, 0).wait_send)
+    for way in (RIGHT, LEFT):
+        sent = out_g.at[pl.ds(0, (hops - 1) * 2 * depth * width // out_g.shape[1])]
+        pltpu.make_async_remote_copy(
+            src_ref=sent, dst_ref=sent, send_sem=send_sem.at[way, 0], recv_sem=recv_sem.at[way, 0],
+            device_id={"zero": toward[way]}, device_id_type=MESH,
+        ).wait_send()
 
     @pl.when(z == 0)
     def _():
-        for k in range(1, nz):
-            to_all(k).wait_send()
+        sent = out_g.at[pl.ds(0, (nz - 1) * out_n.shape[0]), pl.ds(0, out_n.shape[1])]
+        pltpu.make_async_remote_copy(
+            src_ref=sent, dst_ref=sent, send_sem=n_send, recv_sem=n_recv,
+            device_id={"zero": end}, device_id_type=MESH,
+        ).wait_send()
 
     @pl.when(z > 0)
     def _():
@@ -339,14 +365,14 @@
             pltpu.VMEM((lines, 128), F32),
             pltpu.VMEM((nz, lines, 128), F32),
             pltpu.VMEM((nt, nz, lines, 128), F32),
-            dma((6 + len(OWN),)),
-            dma((2, nz // 2, SLOTS)),
-            dma((2, nz // 2, SLOTS)),
-            dma((nt,)),
-            dma((nt,)),
-            dma(()),
-            dma((nz,)),
-            dma((nz,)),
+            dma((6,)),
+            dma((2, 4)),
+            dma((2, SLOTS + 2 * 4 + 3)),
+            dma(()),
+            dma(()),
+            dma(()),
+            dma(()),
+            dma(()),
             dma(()),
             pltpu.SemaphoreType.REGULAR((2,)),
         ],

time: 93.6 us -> 91.9 us (0.982)
  Pallas kernels: 92.7 us -> 91.1 us
    pallas_call x1, Pallas kernels: 89.4 us -> 87.7 us  [body(): pl.pallas_call(functools.partial(ring_kernel, nz, nt), out_shape=(pltpu.V...]
where the time goes in v4:
time: 91.9 us; the launch traced here: 91.7 us
  Pallas kernels  91.1 us (99%)
    pallas_call x1, Pallas kernels, body(): pl.pallas_call(functools.partial(ring_kernel, nz, nt), out_shape=(pltpu.V...  87.7 us
    pallas_call x1, Pallas kernels, body(): pl.pallas_call(store_kernel, out_shape=(jax.ShapeDtypeStruct((width, whol...  3.38 us

profile of v4, /device:TPU:1, one launch (start us, length us, event | category | flops | bytes accessed | tf_op | source)
XLA Modules:
  0.0 91.7 jit_solution(7063849222754533889)
XLA Ops:
  0.6 87.7 %shard_map.103 = (bf16[1024,2048]{1,0:T(8,128)(2,1)S(1)}, bf16[1024,2048]{1,0:T(8,128)(2,1)S(1)}, bf16[16,128]{1,0:T(8,128)(2,1)S(1)}) custom-call(bf16[256,1024]{1,0:T(8,128)(2,1)} %train_g.1, bf16[32,256]{1,0:T(8,128)(2,1)} %bitcast.5, bf16[32,1024]{1,0:T(8,128)(2,1)} %high_g.1, bf16[256,1024]{1,0:T(8,128)(2,1)} %train_u.1, bf16[32,256]{1,0:T(8,128)(2,1)} %bitcast.6, ...), custom_call_target="tpu_custom_call" | custom-call | tf_op jit(solution)/shard_map/pallas_call | solution.py:347
  88.3 3.4 %shard_map.104 = (bf16[1024,2048]{1,0:T(8,128)(2,1)}, bf16[1024,2048]{1,0:T(8,128)(2,1)}, bf16[16,128]{1,0:T(8,128)(2,1)}) custom-call(bf16[1024,2048]{1,0:T(8,128)(2,1)S(1)} %get-tuple-element.9.gate, bf16[1024,2048]{1,0:T(8,128)(2,1)S(1)} %get-tuple-element.10.up, bf16[16,128]{1,0:T(8,128)(2,1)S(1)} %get-tuple-element.11.norm), custom_call_target="tpu_custom_call" | custom-call | tf_op jit(solution)/shard_map/pallas_call | solution.py:383

commit v5 on v4

--- a/solution.py
+++ b/solution.py
@@ -16,12 +16,10 @@
 
 OWN = ((GATE, 0, 2), (GATE, 2, 8), (GATE, 8, 16), (UP, 0, 8), (UP, 8, 16))
 OWN_GATE = 3
-PASSED = (
-    ((GATE, 0, 8), (GATE, 8, 16), (UP, 0, 8), (UP, 8, 16)),
-    ((UP, 0, 8), (UP, 8, 16), (GATE, 0, 8), (GATE, 8, 16)),
-)
+G0, G1, U0, U1 = (GATE, 0, 8), (GATE, 8, 16), (UP, 0, 8), (UP, 8, 16)
+PASSED = (None, ((G0, G1, U0, U1), (G0, U0, G1, U1)), ((G0, G1, U0, U1), (U0, G0, U1, G1)))
 SWAP_GATE, SWAP_UP = (GATE, 11, 16), (UP, 0, 2)
-SLOTS = 5
+SLOTS = len(OWN) + 2 * 4 + 1
 
 
 def ring_kernel(
@@ -29,7 +27,7 @@
     train_g, low_g, high_g, train_u, low_u, high_u, norm_a, norm_b,
     out_g, out_u, out_n,
     tg, tu, lg, lu, hg, hu, na, nb, n_own, n_hub, n_tp,
-    in_sem, send_sem, recv_sem, tp_send, tp_recv, hub_send, hub_recv, n_send, n_recv, go,
+    in_sem, send_sem, recv_sem, sent_sem, came_sem, tp_sem, go,
 ):
     z = lax.axis_index("zero")
     t = lax.axis_index("tp")
@@ -44,12 +42,14 @@
     sources = ((train_g, low_g, high_g), (train_u, low_u, high_u))
     holds = ((tg, lg, hg), (tu, lu, hu))
 
-    loads = {}
-    for p in (GATE, UP):
-        for k in (1, 2):
-            loads[p, k] = pltpu.make_async_copy(
-                sources[p][k], holds[p][k], in_sem.at[k - 1]
-            )
+    head, tail = pl.ds(0, 2 * part), pl.ds(2 * part, 14 * part)
+    first_high = pltpu.make_async_copy(high_g.at[:, head], hg.at[:, head], in_sem.at[1])
+    loads = {
+        (GATE, 1): pltpu.make_async_copy(low_g, lg, in_sem.at[0]),
+        (GATE, 2): pltpu.make_async_copy(high_g.at[:, tail], hg.at[:, tail], in_sem.at[6]),
+        (UP, 1): pltpu.make_async_copy(low_u, lu, in_sem.at[0]),
+        (UP, 2): pltpu.make_async_copy(high_u, hu, in_sem.at[1]),
+    }
     trains = []
     for p, a, b, k in ((GATE, 0, 2, 2), (GATE, 2, 16, 3), (UP, 0, 16, 2)):
         cols = pl.ds(a * part, (b - a) * part)
@@ -60,9 +60,9 @@
         pltpu.make_async_copy(norm_a, na, in_sem.at[4]),
         pltpu.make_async_copy(norm_b, nb, in_sem.at[5]),
     )
+    trains[0].start()
     loads[GATE, 1].start()
-    loads[GATE, 2].start()
-    trains[0].start()
+    first_high.start()
 
     barrier = pltpu.get_barrier_semaphore()
 
@@ -98,6 +98,7 @@
     def _():
         pl.semaphore_signal(go.at[RIGHT], inc=1, device_id={"zero": right}, device_id_type=MESH)
 
+    loads[GATE, 2].start()
     trains[1].start()
     for copy in norm_loads:
         copy.start()
@@ -117,14 +118,17 @@
         base = train[:, cols].T.astype(F32)
         where(z, piece)[...] = (base + mix_rate * mixed).astype(BF16)
 
+    def slot(hop, i):
+        return i if hop == 0 else SLOTS - 1 if hop == hops - 1 else len(OWN) + 4 * (hop - 1) + i
+
     def copy_of(way, hop, i, piece, back):
         gone = hop + back
         origin = lax.rem(z + nz - gone, nz) if way == RIGHT else lax.rem(z + gone, nz)
         block = where(origin, piece)
         return pltpu.make_async_remote_copy(
             src_ref=block, dst_ref=block,
-            send_sem=send_sem.at[way, 0 if hop < hops - 1 else 1 + i],
-            recv_sem=recv_sem.at[way, i if hop == 0 else SLOTS + 4 * (hop - 1) + i],
+            send_sem=send_sem.at[way],
+            recv_sem=recv_sem.at[way, slot(hop, i)],
             device_id={"zero": toward[way]}, device_id_type=MESH,
         )
 
@@ -149,7 +153,7 @@
             copy_of(RIGHT, 0, i, OWN[i], 0).start()
 
     loads[GATE, 1].wait()
-    loads[GATE, 2].wait()
+    first_high.wait()
     trains[0].wait()
     compute(OWN[0])
 
@@ -161,6 +165,7 @@
     loads[UP, 1].start()
     loads[UP, 2].start()
     trains[2].start()
+    loads[GATE, 2].wait()
     trains[1].wait()
     compute(OWN[1])
     first_way(1)
@@ -178,7 +183,7 @@
     mine = (spot >= t * share) & (spot < (t + 1) * share)
     n_own[...] = jnp.where(mine, jnp.broadcast_to(line, shape), 0.0)
     to_hub = pltpu.make_async_remote_copy(
-        src_ref=n_own, dst_ref=n_hub.at[z], send_sem=hub_send, recv_sem=hub_recv,
+        src_ref=n_own, dst_ref=n_hub.at[z], send_sem=sent_sem, recv_sem=came_sem,
         device_id={"zero": 0}, device_id_type=MESH,
     )
 
@@ -208,7 +213,7 @@
 
     def to_all(k):
         return pltpu.make_async_remote_copy(
-            src_ref=out_n, dst_ref=out_n, send_sem=n_send, recv_sem=n_recv,
+            src_ref=out_n, dst_ref=out_n, send_sem=sent_sem, recv_sem=came_sem,
             device_id={"zero": k}, device_id_type=MESH,
         )
 
@@ -218,17 +223,17 @@
         pl.semaphore_wait(barrier, nt - 1)
         rest = n_hub.at[pl.ds(1, nz - 1)]
         pltpu.make_async_remote_copy(
-            src_ref=rest, dst_ref=rest, send_sem=hub_send, recv_sem=hub_recv,
+            src_ref=rest, dst_ref=rest, send_sem=sent_sem, recv_sem=came_sem,
             device_id={"zero": end}, device_id_type=MESH,
         ).wait_recv()
         for d in range(1, nt):
             pltpu.make_async_remote_copy(
-                src_ref=n_hub, dst_ref=n_tp.at[d], send_sem=tp_send, recv_sem=tp_recv,
+                src_ref=n_hub, dst_ref=n_tp.at[d], send_sem=sent_sem, recv_sem=tp_sem,
                 device_id={"tp": lax.rem(t + d, nt)}, device_id_type=MESH,
             ).start()
         rest = n_tp.at[pl.ds(1, nt - 1)]
         pltpu.make_async_remote_copy(
-            src_ref=rest, dst_ref=rest, send_sem=tp_send, recv_sem=tp_recv,
+            src_ref=rest, dst_ref=rest, send_sem=sent_sem, recv_sem=tp_sem,
             device_id={"tp": lax.rem(t + 1, nt)}, device_id_type=MESH,
         ).wait()
         acc = n_hub[...]
@@ -239,7 +244,7 @@
             to_all(k).start()
 
     def pieces_of(way, hop):
-        return OWN if hop == 0 else PASSED[way]
+        return OWN if hop == 0 else PASSED[hop][way]
 
     def last_of(way, dest):
         if way == RIGHT:
@@ -270,9 +275,9 @@
                 copy_of(way, hop, i, pieces_of(way, hop)[i], 1).wait_recv()
 
     for hop in range(1, hops - 1):
-        for i in range(len(PASSED[RIGHT])):
+        for i in range(4):
             for way in (RIGHT, LEFT):
-                piece = PASSED[way][i]
+                piece = PASSED[hop][way][i]
                 land(way, hop - 1, piece)
                 copy_of(way, hop, i, piece, 0).start()
 
@@ -286,27 +291,36 @@
         for p in (GATE, UP):
             land(way, hop - 1, (p, 0, 16))
 
-    for i in range(3):
-        for way in (RIGHT, LEFT):
-            piece, cond = last_of(way, z)[i]
-            guarded(cond, copy_of(way, hop, i, piece, 1).wait_recv)
-
-    for i in range(3):
-        for way in (RIGHT, LEFT):
-            piece, cond = last_of(way, toward[way])[i]
-            guarded(cond, copy_of(way, hop, i, piece, 0).wait_send)
+    swap_gate, swap_up = (p[2] - p[1] for p in (SWAP_GATE, SWAP_UP))
+
+    def total(way, dest, before, act):
+        rows = part * depth // out_g.shape[1]
+        base = before + 16 * rows
+        more, less = (swap_up, swap_gate) if way == RIGHT else (swap_gate, swap_up)
+        gains, loses = (end, 0) if way == RIGHT else (0, end)
+        for cond, count in (
+            (dest == gains, base + more * rows),
+            (dest == loses, base - less * rows),
+            ((dest != gains) & (dest != loses), base),
+        ):
+            block = out_g.at[pl.ds(0, count)]
+            copy = pltpu.make_async_remote_copy(
+                src_ref=block, dst_ref=block,
+                send_sem=send_sem.at[way], recv_sem=recv_sem.at[way, SLOTS - 1],
+                device_id={"zero": toward[way]}, device_id_type=MESH,
+            )
+            pl.when(cond)(functools.partial(act, copy))
+
+    for way in (LEFT, RIGHT):
+        total(way, z, 0, lambda copy: copy.wait_recv())
     for way in (RIGHT, LEFT):
-        sent = out_g.at[pl.ds(0, (hops - 1) * 2 * depth * width // out_g.shape[1])]
-        pltpu.make_async_remote_copy(
-            src_ref=sent, dst_ref=sent, send_sem=send_sem.at[way, 0], recv_sem=recv_sem.at[way, 0],
-            device_id={"zero": toward[way]}, device_id_type=MESH,
-        ).wait_send()
+        total(way, toward[way], (hops - 1) * 2 * depth * width // out_g.shape[1], lambda copy: copy.wait_send())
 
     @pl.when(z == 0)
     def _():
         sent = out_g.at[pl.ds(0, (nz - 1) * out_n.shape[0]), pl.ds(0, out_n.shape[1])]
         pltpu.make_async_remote_copy(
-            src_ref=sent, dst_ref=sent, send_sem=n_send, recv_sem=n_recv,
+            src_ref=sent, dst_ref=sent, send_sem=sent_sem, recv_sem=came_sem,
             device_id={"zero": end}, device_id_type=MESH,
         ).wait_send()
 
@@ -365,12 +379,9 @@
             pltpu.VMEM((lines, 128), F32),
             pltpu.VMEM((nz, lines, 128), F32),
             pltpu.VMEM((nt, nz, lines, 128), F32),
-            dma((6,)),
-            dma((2, 4)),
-            dma((2, SLOTS + 2 * 4 + 3)),
-            dma(()),
-            dma(()),
-            dma(()),
+            dma((7,)),
+            dma((2,)),
+            dma((2, SLOTS)),
             dma(()),
             dma(()),
             dma(()),

time: 91.9 us -> 91.8 us (level)
  no operation moved by 1% of the time
where the time goes in v5:
time: 91.8 us; the launch traced here: 91.6 us
  Pallas kernels  91 us (99%)
    pallas_call x1, Pallas kernels, body(): pl.pallas_call(functools.partial(ring_kernel, nz, nt), out_shape=(pltpu.V...  87.6 us
    pallas_call x1, Pallas kernels, body(): pl.pallas_call(store_kernel, out_shape=(jax.ShapeDtypeStruct((width, whol...  3.38 us

profile of v5, /device:TPU:1, one launch (start us, length us, event | category | flops | bytes accessed | tf_op | source)
XLA Modules:
  0.0 91.6 jit_solution(8558449129855858325)
XLA Ops:
  0.6 87.6 %shard_map.103 = (bf16[1024,2048]{1,0:T(8,128)(2,1)S(1)}, bf16[1024,2048]{1,0:T(8,128)(2,1)S(1)}, bf16[16,128]{1,0:T(8,128)(2,1)S(1)}) custom-call(bf16[256,1024]{1,0:T(8,128)(2,1)} %train_g.1, bf16[32,256]{1,0:T(8,128)(2,1)} %bitcast.5, bf16[32,1024]{1,0:T(8,128)(2,1)} %high_g.1, bf16[256,1024]{1,0:T(8,128)(2,1)} %train_u.1, bf16[32,256]{1,0:T(8,128)(2,1)} %bitcast.6, ...), custom_call_target="tpu_custom_call" | custom-call | tf_op jit(solution)/shard_map/pallas_call | solution.py:361
  88.2 3.4 %shard_map.104 = (bf16[1024,2048]{1,0:T(8,128)(2,1)}, bf16[1024,2048]{1,0:T(8,128)(2,1)}, bf16[16,128]{1,0:T(8,128)(2,1)}) custom-call(bf16[1024,2048]{1,0:T(8,128)(2,1)S(1)} %get-tuple-element.9.gate, bf16[1024,2048]{1,0:T(8,128)(2,1)S(1)} %get-tuple-element.10.up, bf16[16,128]{1,0:T(8,128)(2,1)S(1)} %get-tuple-element.11.norm), custom_call_target="tpu_custom_call" | custom-call | tf_op jit(solution)/shard_map/pallas_call | solution.py:394

commit v6 on v5

--- a/solution.py
+++ b/solution.py
@@ -18,7 +18,7 @@
 OWN_GATE = 3
 G0, G1, U0, U1 = (GATE, 0, 8), (GATE, 8, 16), (UP, 0, 8), (UP, 8, 16)
 PASSED = (None, ((G0, G1, U0, U1), (G0, U0, G1, U1)), ((G0, G1, U0, U1), (U0, G0, U1, G1)))
-SWAP_GATE, SWAP_UP = (GATE, 11, 16), (UP, 0, 2)
+SWAP_GATE, SWAP_UP = (GATE, 11, 16), (UP, 0, 3)
 SLOTS = len(OWN) + 2 * 4 + 1
 
 
@@ -331,13 +331,11 @@
 
 
 def store_kernel(gate, up, norm, out_g, out_u, out_n, sem):
-    copies = []
-    rows = gate.shape[0] // 4
-    for k in range(4):
-        part = pl.ds(k * rows, rows)
-        copies.append(pltpu.make_async_copy(gate.at[part], out_g.at[part], sem.at[2 * k]))
-        copies.append(pltpu.make_async_copy(up.at[part], out_u.at[part], sem.at[2 * k + 1]))
-    copies.append(pltpu.make_async_copy(norm, out_n, sem.at[8]))
+    copies = (
+        pltpu.make_async_copy(gate, out_g, sem.at[0]),
+        pltpu.make_async_copy(up, out_u, sem.at[1]),
+        pltpu.make_async_copy(norm, out_n, sem.at[2]),
+    )
     for copy in copies:
         copy.start()
     for copy in copies:
@@ -400,7 +398,7 @@
         ),
         in_specs=[vmem] * 3,
         out_specs=(hbm,) * 3,
-        scratch_shapes=[dma((9,))],
+        scratch_shapes=[dma((3,))],
         compiler_params=pltpu.CompilerParams(vmem_limit_bytes=24 * 1024 * 1024),
     )(gate, up, norm)
     return gate, up, norm.reshape(whole)

time: 91.8 us -> 91.6 us (level)
  no operation moved by 1% of the time
where the time goes in v6:
time: 91.6 us; the launch traced here: 91.4 us
  Pallas kernels  90.8 us (99%)
    pallas_call x1, Pallas kernels, body(): pl.pallas_call(functools.partial(ring_kernel, nz, nt), out_shape=(pltpu.V...  87.3 us
    pallas_call x1, Pallas kernels, body(): pl.pallas_call(store_kernel, out_shape=(jax.ShapeDtypeStruct((width, whol...  3.42 us

profile of v6, /device:TPU:1, one launch (start us, length us, event | category | flops | bytes accessed | tf_op | source)
XLA Modules:
  0.0 91.4 jit_solution(13358386477907957736)
XLA Ops:
  0.6 87.3 %shard_map.103 = (bf16[1024,2048]{1,0:T(8,128)(2,1)S(1)}, bf16[1024,2048]{1,0:T(8,128)(2,1)S(1)}, bf16[16,128]{1,0:T(8,128)(2,1)S(1)}) custom-call(bf16[256,1024]{1,0:T(8,128)(2,1)} %train_g.1, bf16[32,256]{1,0:T(8,128)(2,1)} %bitcast.5, bf16[32,1024]{1,0:T(8,128)(2,1)} %high_g.1, bf16[256,1024]{1,0:T(8,128)(2,1)} %train_u.1, bf16[32,256]{1,0:T(8,128)(2,1)} %bitcast.6, ...), custom_call_target="tpu_custom_call" | custom-call | tf_op jit(solution)/shard_map/pallas_call | solution.py:359
  88.0 3.4 %shard_map.104 = (bf16[1024,2048]{1,0:T(8,128)(2,1)}, bf16[1024,2048]{1,0:T(8,128)(2,1)}, bf16[16,128]{1,0:T(8,128)(2,1)}) custom-call(bf16[1024,2048]{1,0:T(8,128)(2,1)S(1)} %get-tuple-element.9.gate, bf16[1024,2048]{1,0:T(8,128)(2,1)S(1)} %get-tuple-element.10.up, bf16[16,128]{1,0:T(8,128)(2,1)S(1)} %get-tuple-element.11.norm), custom_call_target="tpu_custom_call" | custom-call | tf_op jit(solution)/shard_map/pallas_call | solution.py:392

commit v7 on v6

--- a/solution.py
+++ b/solution.py
@@ -19,7 +19,8 @@
 G0, G1, U0, U1 = (GATE, 0, 8), (GATE, 8, 16), (UP, 0, 8), (UP, 8, 16)
 PASSED = (None, ((G0, G1, U0, U1), (G0, U0, G1, U1)), ((G0, G1, U0, U1), (U0, G0, U1, G1)))
 SWAP_GATE, SWAP_UP = (GATE, 11, 16), (UP, 0, 3)
-SLOTS = len(OWN) + 2 * 4 + 1
+SLOTS = len(OWN) + 4 + 1
+AGAIN, LAST_SLOT = ((SLOTS - 1, 0, 1, 2), (SLOTS - 1, 0, 1, 3)), (3, 2)
 
 
 def ring_kernel(
@@ -108,18 +109,26 @@
         first = pl.multiple_of(origin * depth, depth)
         return outs[p].at[pl.ds(a * part, (b - a) * part), pl.ds(first, depth)]
 
-    def compute(piece):
+    def mix(piece):
         p, a, b = piece
         train, low, high = holds[p]
-        cols = pl.ds(a * part, (b - a) * part)
-        mixed = lax.dot_general(
-            high[:, cols], low[...], (((0,), (0,)), ((), ())), preferred_element_type=F32
-        )
-        base = train[:, cols].T.astype(F32)
-        where(z, piece)[...] = (base + mix_rate * mixed).astype(BF16)
-
-    def slot(hop, i):
-        return i if hop == 0 else SLOTS - 1 if hop == hops - 1 else len(OWN) + 4 * (hop - 1) + i
+        return mix_rate * lax.dot_general(
+            high[:, pl.ds(a * part, (b - a) * part)], low[...],
+            (((0,), (0,)), ((), ())), preferred_element_type=F32,
+        )
+
+    def merge(piece, mixed):
+        p, a, b = piece
+        base = holds[p][0][:, pl.ds(a * part, (b - a) * part)].T.astype(F32)
+        where(z, piece)[...] = (base + mixed).astype(BF16)
+
+    def compute(piece):
+        merge(piece, mix(piece))
+
+    def slot(way, hop, i):
+        if hop < 2:
+            return len(OWN) * hop + i
+        return AGAIN[way][i] if hop < hops - 1 else LAST_SLOT[way]
 
     def copy_of(way, hop, i, piece, back):
         gone = hop + back
@@ -128,7 +137,7 @@
         return pltpu.make_async_remote_copy(
             src_ref=block, dst_ref=block,
             send_sem=send_sem.at[way],
-            recv_sem=recv_sem.at[way, slot(hop, i)],
+            recv_sem=recv_sem.at[way, slot(way, hop, i)],
             device_id={"zero": toward[way]}, device_id_type=MESH,
         )
 
@@ -154,8 +163,9 @@
 
     loads[GATE, 1].wait()
     first_high.wait()
+    mixed = mix(OWN[0])
     trains[0].wait()
-    compute(OWN[0])
+    merge(OWN[0], mixed)
 
     @pl.when(z == 0)
     def _():
@@ -306,7 +316,7 @@
             block = out_g.at[pl.ds(0, count)]
             copy = pltpu.make_async_remote_copy(
                 src_ref=block, dst_ref=block,
-                send_sem=send_sem.at[way], recv_sem=recv_sem.at[way, SLOTS - 1],
+                send_sem=send_sem.at[way], recv_sem=recv_sem.at[way, LAST_SLOT[way]],
                 device_id={"zero": toward[way]}, device_id_type=MESH,
             )
             pl.when(cond)(functools.partial(act, copy))

time: 91.6 us -> 91.5 us (level)
  no operation moved by 1% of the time
where the time goes in v7:
time: 91.5 us; the launch traced here: 91.3 us
  Pallas kernels  90.7 us (99%)
    pallas_call x1, Pallas kernels, body(): pl.pallas_call(functools.partial(ring_kernel, nz, nt), out_shape=(pltpu.V...  87.3 us
    pallas_call x1, Pallas kernels, body(): pl.pallas_call(store_kernel, out_shape=(jax.ShapeDtypeStruct((width, whol...  3.42 us

profile of v7, /device:TPU:1, one launch (start us, length us, event | category | flops | bytes accessed | tf_op | source)
XLA Modules:
  0.0 91.3 jit_solution(8296878466147376932)
XLA Ops:
  0.6 87.3 %shard_map.103 = (bf16[1024,2048]{1,0:T(8,128)(2,1)S(1)}, bf16[1024,2048]{1,0:T(8,128)(2,1)S(1)}, bf16[16,128]{1,0:T(8,128)(2,1)S(1)}) custom-call(bf16[256,1024]{1,0:T(8,128)(2,1)} %train_g.1, bf16[32,256]{1,0:T(8,128)(2,1)} %bitcast.5, bf16[32,1024]{1,0:T(8,128)(2,1)} %high_g.1, bf16[256,1024]{1,0:T(8,128)(2,1)} %train_u.1, bf16[32,256]{1,0:T(8,128)(2,1)} %bitcast.6, ...), custom_call_target="tpu_custom_call" | custom-call | tf_op jit(solution)/shard_map/pallas_call | solution.py:369
  87.9 3.4 %shard_map.104 = (bf16[1024,2048]{1,0:T(8,128)(2,1)}, bf16[1024,2048]{1,0:T(8,128)(2,1)}, bf16[16,128]{1,0:T(8,128)(2,1)}) custom-call(bf16[1024,2048]{1,0:T(8,128)(2,1)S(1)} %get-tuple-element.9.gate, bf16[1024,2048]{1,0:T(8,128)(2,1)S(1)} %get-tuple-element.10.up, bf16[16,128]{1,0:T(8,128)(2,1)S(1)} %get-tuple-element.11.norm), custom_call_target="tpu_custom_call" | custom-call | tf_op jit(solution)/shard_map/pallas_call | solution.py:402
